TPU v7x, 256 devices: a whole 4x4x8 slice. The times are simulated.
256 devices in a mesh: dp: 32 (over x, z), col: 8 (over y, core).
Axes of the slice: x: 4, y: 4, z: 8, core: 2. Of those that a mesh axis runs over, the one named last changes fastest.
Arguments:
- activations: bfloat16 [2, 28672, 8192], P(None, 'dp', 'col'), may hold values from -40 to 40
- cotangent: bfloat16 [2, 28672, 2048], P(None, 'dp'), may hold values from -40 to 40
- master_weights: float32 [2, 2048, 8192], P(None, 'dp', 'col'), may hold values from -6 to 6
- moment_codes: bfloat16 [2, 2048, 8192], P(None, 'dp', 'col'), may hold values from -1 to 1
- square_codes: bfloat16 [2, 2048, 8192], P(None, 'dp', 'col'), may hold values from 0.049804688 to 1
- moment_scales: float32 [2, 2048, 4], P(None, 'dp'), may hold values from 0.05 to 0.5
- square_scales: float32 [2, 2048, 4], P(None, 'dp'), may hold values from 0.005 to 0.05
Outputs:
- new_weights: float32 [2, 2048, 8192], P(None, 'dp', 'col')
- new_moment_codes: bfloat16 [2, 2048, 8192], P(None, 'dp', 'col')
- new_square_codes: bfloat16 [2, 2048, 8192], P(None, 'dp', 'col')
- new_moment_scales: float32 [2, 2048, 4], P(None, 'dp')
- new_square_scales: float32 [2, 2048, 4], P(None, 'dp')
All inputs are finite; a program needn't handle non-finite values. Where the computation divides by a largest or mean magnitude, that divisor is 1e-20 or more.
Results may differ from a plain program's by a relative error of at most 0.001.
Values sent between devices are 32-bit elements; how exact they have to be, the bound alone decides.
A program may use at most 128 MiB of HBM per device.

v0:
```python
import jax
import jax.numpy as jnp
from jax import lax
from jax.sharding import Mesh
from jax.sharding import PartitionSpec as P

D = 8192
KV = 2048
BLOCK = 2048
LAYERS = 2
STEP = 10
DP = ("dp_0", "dp_1")
DP_COL = ("dp_0", "dp_1", "col_0", "col_1")
COL = ("col_0", "col_1")


beta_one = 0.9
beta_two = 0.999
learn_rate = 0.001
decay_rate = 0.1
adam_eps = 1e-08
scale_eps = 1e-06
norm_eps = 1e-06


def summed_rows(total, axes):
    for axis in axes:
        total = lax.psum_scatter(total, axis, scatter_dimension=0, tiled=True)
    return total


def by_axis(array, axes):
    for axis in axes:
        array = lax.psum(array, axis)
    return array


def sent_to_all(array, axis):
    copies = jnp.broadcast_to(array, (lax.axis_size(axis), *array.shape))
    return lax.all_to_all(copies, axis, split_axis=0, concat_axis=0, tiled=True)


def over_copies(array, axis):
    everything = sent_to_all(array, axis)
    return jnp.max(everything, axis=0)


def packed_total(arrays, axis):
    line, at, outs = (jnp.concatenate([a.reshape(-1) for a in arrays]), 0, [])
    total = over_copies(line, axis)
    for a in arrays:
        outs.append(total[at : at + a.size].reshape(a.shape))
        at += a.size
    return tuple(outs)


def local(
    activations, cotangent, master_weights, moment_codes, square_codes, moment_scales, square_scales
):
    layer_count = activations.shape[0]
    shard_cols = master_weights.shape[2]
    block_count = moment_scales.shape[2]
    summed = summed_rows(
        jnp.einsum("ltk,ltd->kld", cotangent, activations, preferred_element_type=jnp.float32), DP
    )
    gradient = jnp.transpose(summed, (1, 0, 2))
    local_sq = jnp.sum(gradient * gradient)
    total_sq = by_axis(local_sq, DP_COL)
    rms = jnp.sqrt(total_sq / float(LAYERS * KV * D) + norm_eps)
    clip_factor = jnp.minimum(1.0, 1.0 / rms)
    correct_one = 1.0 - beta_one**STEP
    correct_two = 1.0 - beta_two**STEP
    own_block = lax.axis_index(COL) * shard_cols // BLOCK
    selector = (jnp.arange(block_count, dtype=jnp.int32) == own_block).astype(jnp.float32)

    def new_moments(layer_index):
        moment_scale = jnp.sum(moment_scales[layer_index] * selector, axis=1)
        square_scale = jnp.sum(square_scales[layer_index] * selector, axis=1)
        old_moment = moment_codes[layer_index].astype(jnp.float32) * moment_scale[:, None]
        old_square = square_codes[layer_index].astype(jnp.float32) * square_scale[:, None]
        grad_now = clip_factor * gradient[layer_index]
        moment = beta_one * old_moment + (1.0 - beta_one) * grad_now
        square = beta_two * old_square + (1.0 - beta_two) * grad_now * grad_now
        moment_part = jnp.max(jnp.abs(moment), axis=1)[:, None] * selector
        square_part = jnp.max(square, axis=1)[:, None] * selector
        return (moment, square, moment_part, square_part)

    outs_weights, outs_mcode, outs_scode, outs_mscale, outs_sscale = ([], [], [], [], [])
    states = [new_moments(layer_index) for layer_index in range(layer_count)]
    moment_maxima, square_maxima = packed_total(
        (jnp.stack([state[2] for state in states]), jnp.stack([state[3] for state in states])), COL
    )
    for layer_index in range(layer_count):
        moment, square = (states[layer_index][0], states[layer_index][1])
        moment_max = moment_maxima[layer_index]
        square_max = square_maxima[layer_index]
        moment_div = jnp.sum(moment_max * selector, axis=1)[:, None]
        square_div = jnp.sum(square_max * selector, axis=1)[:, None]
        moment_out = (moment / (moment_div + scale_eps)).astype(jnp.bfloat16)
        square_out = (square / (square_div + scale_eps)).astype(jnp.bfloat16)
        ratio = moment / correct_one / (jnp.sqrt(square / correct_two) + adam_eps)
        weights = master_weights[layer_index]
        results = (weights - learn_rate * (decay_rate * weights + ratio), moment_out, square_out)
        outs_weights.append(results[0])
        outs_mcode.append(results[1])
        outs_scode.append(results[2])
        outs_mscale.append(moment_maxima[layer_index])
        outs_sscale.append(square_maxima[layer_index])
    return (
        jnp.stack(outs_weights),
        jnp.stack(outs_mcode),
        jnp.stack(outs_scode),
        jnp.stack(outs_mscale),
        jnp.stack(outs_sscale),
    )


def solution(mesh):
    split = Mesh(mesh.devices.reshape(4, 8, 4, 2), ("dp_0", "dp_1", "col_0", "col_1"))
    in_specs = (
        P(None, DP, COL),
        P(None, DP, None),
        P(None, DP, COL),
        P(None, DP, COL),
        P(None, DP, COL),
        P(None, DP, None),
        P(None, DP, None),
    )
    out_specs = (
        P(None, DP, COL),
        P(None, DP, COL),
        P(None, DP, COL),
        P(None, DP, None),
        P(None, DP, None),
    )
    return jax.shard_map(local, mesh=split, in_specs=in_specs, out_specs=out_specs, check_vma=False)
```

profile of v0, /device:TPU:1, one launch (start us, length us, event | category | flops | bytes accessed | tf_op | source)
XLA Modules:
  0.0 359.9 jit_solution(13707832708367984324)
XLA Ops:
  7.2 16.0 %convolution_bitcast_fusion = f32[2048,2,1024]{0,2,1:T(8,128)} fusion(bf16[2,896,1024]{2,1,0:T(8,128)(2,1)} %param.7, bf16[2,896,2048]{2,1,0:T(8,128)(2,1)} %param.8), kind=kOutput, calls=%fused_computation | convolution fusion | flops 7516192768 | bytes 27787264 | tf_op jit(solution)/shard_map/ltk,ltd->kld/dot_general | solution.py:64
  23.3 154.3 %reduce-scatter.2.cloned.1.call-done = f32[512,2,1024]{0,2,1:T(8,128)} async-done(((f32[2048,2,1024]{0,2,1:T(8,128)}), f32[512,2,1024]{0,2,1:T(8,128)}) %reduce-scatter.2.cloned.1.call-update) | async-done | bytes 4194320 | tf_op jit(solution)/shard_map/reduce_scatter | solution.py:28
  177.6 7.4 %copy.92 = f32[512,2,1024]{2,1,0:T(2,128)} copy(f32[512,2,1024]{0,2,1:T(8,128)} %reduce-scatter.2.cloned.1.call-done) | data formatting | bytes 8388608 | tf_op jit(solution)/shard_map/reduce_scatter | solution.py:28
  185.1 0.6 copy-done.3
  185.9 0.6 dynamic-slice
  187.1 106.7 %all-reduce.3.cloned.1.call-done = f32[512,2,1024]{2,1,0:T(2,128)} async-done(((f32[512,2,1024]{2,1,0:T(2,128)}), f32[512,2,1024]{2,1,0:T(2,128)}) %all-reduce.3.cloned.1.call-update) | async-done | bytes 4194320
  293.8 1.1 constant_dynamic-slice_fusion
  294.9 0.7 multiply_reduce_fusion
  295.7 9.0 %psum.28 = f32[]{:T(128)} all-reduce(f32[]{:T(128)} %multiply_reduce_fusion), channel_id=1, replica_groups=mesh['dp_0'=4,'dp_1'=8,'col_0'=4,'col_1'=2] {'dp_0'}, use_global_device_ids=true, to_apply=%region_4.0 | all-reduce | flops 1 | bytes 8 | tf_op jit(solution)/shard_map/psum | solution.py:34
  304.8 12.4 %psum.29 = f32[]{:T(128)} all-reduce(f32[]{:T(128)} %psum.28), channel_id=1, replica_groups=mesh['dp_0'=4,'dp_1'=8,'col_0'=4,'col_1'=2] {'dp_1'}, use_global_device_ids=true, to_apply=%region_5.0 | all-reduce | flops 1 | bytes 8 | tf_op jit(solution)/shard_map/psum | solution.py:34
  317.2 0.1 fusion.28
  317.4 9.1 %psum.30 = f32[]{:T(128)} all-reduce(f32[]{:T(128)} %psum.29), channel_id=1, replica_groups=mesh['dp_0'=4,'dp_1'=8,'col_0'=4,'col_1'=2] {'col_0'}, use_global_device_ids=true, to_apply=%region_6.0 | all-reduce | flops 1 | bytes 8 | tf_op jit(solution)/shard_map/psum | solution.py:34
  326.5 0.2 copy.117
  326.6 11.4 %psum.31 = f32[]{:T(128)} all-reduce(f32[]{:T(128)} %psum.30), channel_id=1, replica_groups=mesh['dp_0'=4,'dp_1'=8,'col_0'=4,'col_1'=2] {'col_1'}, use_global_device_ids=true, to_apply=%region_7.8 | all-reduce | flops 1 | bytes 8 | tf_op jit(solution)/shard_map/psum | solution.py:34
  338.8 0.5 fusion.6
  339.3 0.1 copy.98
  339.4 0.1 reshape.364
  339.5 0.1 copy.97
  339.6 0.1 reshape.363
  339.8 7.4 %all_to_all.6 = f32[8,1,1024]{2,1,0:T(1,128)S(1)} all-to-all(f32[8,1,1024]{2,1,0:T(1,128)S(1)} %broadcast_in_dim.2), channel_id=1, replica_groups=mesh['dp_0'=4,'dp_1'=8,'col_0'=4,'col_1'=2] {'col_0','col_1'}, dimensions={0} | all-to-all | bytes 65536 | tf_op jit(solution)/shard_map/all_to_all | solution.py:40
  347.3 0.1 slice.157
  347.4 0.1 slice.163
  347.5 0.1 slice.155
  347.6 0.1 slice.162
  348.1 0.2 multiply_reduce_fusion.2
  348.6 0.8 multiply_subtract_fusion.1
  349.4 0.8 pad_maximum_fusion
  350.2 0.2 divide_convert_fusion.1
  350.4 0.7 pad_maximum_fusion.1
  351.2 0.7 pad_maximum_fusion.2
  351.9 0.6 pad_maximum_fusion.6
  352.5 0.6 pad_maximum_fusion.7
  (40 shorter events, 1.4 us)
Async XLA Ops:
  7.2 170.4 %reduce-scatter.2.cloned.1.call-start = ((), (), s32[]{:S(2)}) async-start(), calls=%async_computation.2 | async-start | bytes 20971520 | tf_op jit(solution)/shard_map/reduce_scatter | solution.py:28
  23.3 270.6 %all-reduce.3.cloned.1.call-start = ((), (), s32[]{:S(2)}) async-start(), calls=%async_computation.3 | async-start | bytes 8388608
  185.0 0.7 copy-start.3
  185.0 0.8 copy-start.4
  185.0 0.9 copy-start.5
  185.0 153.8 %copy-start = (bf16[2,64,1024]{2,1,0:T(8,128)(2,1)S(1)}, bf16[2,64,1024]{2,1,0:T(8,128)(2,1)}, u32[]{:S(2)}) copy-start(bf16[2,64,1024]{2,1,0:T(8,128)(2,1)} %param.10) | copy-start | bytes 786436
  185.0 153.8 %copy-start.1 = (bf16[2,64,1024]{2,1,0:T(8,128)(2,1)S(1)}, bf16[2,64,1024]{2,1,0:T(8,128)(2,1)}, u32[]{:S(2)}) copy-start(bf16[2,64,1024]{2,1,0:T(8,128)(2,1)} %param.11) | copy-start | bytes 786436
  185.0 163.6 %copy-start.2 = (f32[2,64,1024]{2,1,0:T(8,128)S(1)}, f32[2,64,1024]{2,1,0:T(8,128)}, u32[]{:S(2)}) copy-start(f32[2,64,1024]{2,1,0:T(8,128)} %param.9) | copy-start | bytes 1572868
Sparse Core Ops, SparseCore 0:
  23.4 154.1 reduce-scatter.1
  185.2 108.6 all-reduce.2
where the time goes:
time: 360 us
  waiting for transfers between devices  261 us (72%)
  blocking collectives  49.3 us (14%)
  matrix products  16 us (4%)
  between operations  15.6 us (4%)
  local copies, waits for them, and re-layouts  11.8 us (3%)
  other arithmetic  6.09 us (2%)
    reduce_scatter x1, waiting for transfers between devices, summed_rows(): total = lax.psum_scatter(total, axis, scatter_dimension=0, tiled=True)  154 us
    unnamed x3, waiting for transfers between devices  107 us
    psum x4, blocking collectives, by_axis(): array = lax.psum(array, axis)  41.9 us
    dot_general x1, matrix products, local(): jnp.einsum('ltk,ltd->kld', cotangent, activations, preferred_element_type...  16 us
    reduce_scatter x2, local copies, waits for them, and re-layouts, summed_rows(): total = lax.psum_scatter(total, axis, scatter_dimension=0, tiled=True)  7.54 us
    all_to_all x1, blocking collectives, sent_to_all(): return lax.all_to_all(copies, axis, split_axis=0, concat_axis=0, tiled=True)  7.43 us
  transfers between devices with their start and end apart: 2, of which 2 were waited for; matrix products, arithmetic and copies ran while one was open for 0% of the time, Pallas kernels for 0%

commit v1 on v0

v1 whole, which is shorter than its diff:
```python
import functools
import heapq

import jax
import jax.numpy as jnp
from jax import lax
from jax.experimental import pallas as pl
from jax.experimental.pallas import tpu as pltpu
from jax.sharding import Mesh
from jax.sharding import PartitionSpec as P

D = 8192
KV = 2048
BLOCK = 2048
LAYERS = 2
STEP = 10

beta_one = 0.9
beta_two = 0.999
learn_rate = 0.001
decay_rate = 0.1
adam_eps = 1e-08
scale_eps = 1e-06
norm_eps = 1e-06

NX, NZ, NY, NC = 4, 8, 4, 2
ROWS = KV // (NX * NZ)
COLS = D // (NY * NC)
TOK = 896
XROWS = ROWS * NZ
CA = 640
CB = COLS - CA
WINDOW_A, WINDOW_B = 3, 2
NT = 512
MESH = pl.DeviceIdType.MESH
F32 = jnp.float32


def task_order(rate=46.6e3, latency=2.3, add=0.1, matmul=2.0):
    bytes_a, bytes_b = ROWS * CA * 4, ROWS * CB * 4
    now, order, free, heap, seen = 0.0, [], {}, [], set()
    matmuls = [("M", d, s, 0) for s in range(NX) for d in (0, 1)]
    arrived, count, serial = [], 0, 0
    total = 2 * (NZ * (NX - 1) + NZ - 1 + NX * (NZ - 1) + NX - 1)

    def ready(task):
        kind, d, j, s = task
        need = {
            "A": ("M", d, s + 1, 0),
            "B": ("M", d, j, 0),
            "ZA": ("A", d, s + 1, NX - 2),
            "XB": ("B", d, j + 1, NZ - 2),
        }[kind]
        return need in seen

    def enabled(task):
        kind, d, j, s = task
        out = []
        if kind == "M":
            if j == 0:
                out += [("A", d, q, 0) for q in range(WINDOW_A)]
            if j < WINDOW_B:
                out.append(("B", d, j, 0))
        elif kind == "A":
            if s < NX - 2:
                out.append(("A", d, j, s + 1))
            else:
                if j == 0:
                    out.append(("ZA", d, 0, 0))
                if j + WINDOW_A < NZ:
                    out.append(("A", d, j + WINDOW_A, 0))
        elif kind == "B":
            if s < NZ - 2:
                out.append(("B", d, j, s + 1))
            else:
                if j == 0:
                    out.append(("XB", d, 0, 0))
                if j + WINDOW_B < NX:
                    out.append(("B", d, j + WINDOW_B, 0))
        elif kind == "ZA":
            if s < NZ - 2:
                out.append(("ZA", d, 0, s + 1))
        elif kind == "XB":
            if j < NX - 2:
                out.append(("XB", d, j + 1, 0))
        return out

    while count < total or matmuls:
        while heap and heap[0][0] <= now:
            arrived.append(heapq.heappop(heap))
        able = [a for a in arrived if ready(a[2])]
        if able:
            first = min(able)
            arrived.remove(first)
            task = first[2]
            now += add
            count += 1
        elif matmuls:
            task = matmuls.pop(0)
            now += matmul
        else:
            now = max(now, heap[0][0])
            continue
        seen.add(task)
        sends = enabled(task)
        for send in sends:
            link = ("x" if send[0] in ("A", "XB") else "z", send[1])
            size = bytes_a if send[0] in ("A", "ZA") else bytes_b
            free[link] = max(now, free.get(link, 0.0)) + size / rate
            heapq.heappush(heap, (free[link] + latency, serial, send))
            serial += 1
        order.append((task, sends))
    return order


def kernel(
    act_hbm, cot_hbm, master_hbm, mcode_hbm, scode_hbm, mscale_hbm, sscale_hbm,
    weights_out, mcode_out, scode_out, mscale_out, sscale_out,
    act, cot, master, mcode, scode, mscale, sscale,
    part, buf_a, buf_za, buf_b, buf_xb, grad, mom, sqr, norm_send, norm_recv, top_send, top_recv, gather,
    in_sems, send_a, recv_a, send_za, recv_za, send_b, recv_b, send_xb, recv_xb,
    norm_send_sems, norm_recv_sems, top_sems, gather_send_sems, gather_recv_sems,
):
    x, z, y, c = (lax.axis_index(n) for n in ("x", "z", "y", "core"))
    sign = (1, -1)

    def wrap(v, n):
        return lax.rem(v + 2 * n, n)

    def xrel(d, s):
        return wrap(x - sign[d] * (1 + s), NX)

    def zrel(d, s):
        return wrap(z - sign[d] * (1 + s), NZ)

    loads = {}

    def load(name, src, dst, k):
        loads[name] = pltpu.make_async_copy(src, dst, in_sems.at[k])
        loads[name].start()

    def cot_columns(d, s):
        return pl.ds(pl.multiple_of(xrel(d, s) * XROWS, XROWS), XROWS)

    k = 0
    for s in range(NX):
        for d in (0, 1):
            if s == 0:
                load(("act", d), act_hbm.at[d], act.at[d], k)
                k += 1
            load(("cot", d, s), cot_hbm.at[d, :, cot_columns(d, s)], cot.at[d, s], k)
            k += 1
    for name, src, dst in (
        ("master", master_hbm, master), ("mcode", mcode_hbm, mcode), ("scode", scode_hbm, scode),
        ("mscale", mscale_hbm, mscale), ("sscale", sscale_hbm, sscale),
    ):
        load(name, src, dst, k)
        k += 1

    col_peers = [(dy, dc) for dy in range(NY) for dc in range(NC) if dy or dc]
    barrier = pltpu.get_barrier_semaphore()
    peers = (
        [{"x": wrap(x + i, NX)} for i in range(1, NX)]
        + [{"z": wrap(z + i, NZ)} for i in range(1, NZ)]
        + [{"y": wrap(y + dy, NY), "core": wrap(c + dc, NC)} for dy, dc in col_peers]
    )
    for peer in peers:
        pl.semaphore_signal(barrier, inc=1, device_id=peer, device_id_type=MESH)

    def rows_z(d, j):
        return pl.ds(pl.multiple_of(zrel(d, j) * ROWS, ROWS), ROWS)

    def own_a(d, j, s):
        return part.at[d, s, rows_z(d, j), pl.ds(0, CA)]

    def own_b(d, j, s):
        return part.at[d, j, rows_z(d, s), pl.ds(CA, CB)]

    def copy_of(task):
        kind, d, j, s = task
        if kind == "A":
            i = j * (NX - 1) + s
            src = own_a(d, j, 0) if s == 0 else buf_a.at[d, i - 1]
            dst, ssem, rsem, axis = buf_a.at[d, i], send_a.at[d, i], recv_a.at[d, i], "x"
        elif kind == "ZA":
            src = buf_a.at[d, NX - 2] if s == 0 else buf_za.at[d, s - 1]
            dst, ssem, rsem, axis = buf_za.at[d, s], send_za.at[d, s], recv_za.at[d, s], "z"
        elif kind == "B":
            i = j * (NZ - 1) + s
            src = own_b(d, j, 0) if s == 0 else buf_b.at[d, i - 1]
            dst, ssem, rsem, axis = buf_b.at[d, i], send_b.at[d, i], recv_b.at[d, i], "z"
        else:
            src = buf_b.at[d, NZ - 2] if j == 0 else buf_xb.at[d, j - 1]
            dst, ssem, rsem, axis = buf_xb.at[d, j], send_xb.at[d, j], recv_xb.at[d, j], "x"
        target = wrap(x + sign[d], NX) if axis == "x" else wrap(z + sign[d], NZ)
        return pltpu.make_async_remote_copy(
            src_ref=src, dst_ref=dst, send_sem=ssem, recv_sem=rsem,
            device_id={axis: target}, device_id_type=MESH,
        )

    def add_own(task):
        kind, d, j, s = task
        if kind == "A":
            i = j * (NX - 1) + s
            buf_a[d, i] = buf_a[d, i] + own_a(d, j, s + 1)[...]
        elif kind == "ZA":
            mine = buf_a[d, (s + 1) * (NX - 1) + NX - 2]
            if s == NZ - 2:
                grad[d, :, :CA] = buf_za[d, s] + mine
            else:
                buf_za[d, s] = buf_za[d, s] + mine
        elif kind == "B":
            i = j * (NZ - 1) + s
            buf_b[d, i] = buf_b[d, i] + own_b(d, j, s + 1)[...]
        else:
            mine = buf_b[d, (j + 1) * (NZ - 1) + NZ - 2]
            if j == NX - 2:
                grad[d, :, CA:] = buf_xb[d, j] + mine
            else:
                buf_xb[d, j] = buf_xb[d, j] + mine

    def matmul(d, s):
        if s == 0:
            loads[("act", d)].wait()
        loads[("cot", d, s)].wait()

        @pl.loop(0, COLS // NT)
        def _(n):
            cols = pl.ds(pl.multiple_of(n * NT, NT), NT)
            part[d, s, :, cols] = lax.dot_general(
                cot[d, s], act[d, :, cols], (((0,), (0,)), ((), ())), preferred_element_type=F32
            )

    started = []
    first = True
    for task, sends in task_order():
        if task[0] == "M":
            matmul(task[1], task[2])
            if first:
                pl.semaphore_wait(barrier, len(peers))
                first = False
        else:
            copy_of(task).wait_recv()
            add_own(task)
        for send in sends:
            copy = copy_of(send)
            copy.start()
            started.append(copy)

    total = jnp.zeros((8, 128), F32)
    for d in range(LAYERS):
        for r in range(ROWS // 8):
            v = grad[d, pl.ds(r * 8, 8), :]
            v = v * v
            for i in range(COLS // 128):
                total = total + v[:, i * 128 : (i + 1) * 128]
    line = jnp.sum(total, axis=0, keepdims=True)
    stages = (
        [({"y": wrap(y + dy, NY), "core": wrap(c + dc, NC)}) for dy, dc in col_peers],
        [{"x": wrap(x + i, NX)} for i in range(1, NX)],
        [{"z": wrap(z + i, NZ)} for i in range(1, NZ)],
    )
    base = 0
    for n, stage in enumerate(stages):
        norm_send[n] = line
        copies = []
        for i, peer in enumerate(stage):
            copy = pltpu.make_async_remote_copy(
                src_ref=norm_send.at[n], dst_ref=norm_recv.at[base + i],
                send_sem=norm_send_sems.at[base + i], recv_sem=norm_recv_sems.at[base + i],
                device_id=peer, device_id_type=MESH,
            )
            copy.start()
            copies.append(copy)
        for i, copy in enumerate(copies):
            copy.wait_recv()
            line = line + norm_recv[base + i]
        started += copies
        base += len(stage)
    total_sq = jnp.sum(line, axis=1, keepdims=True)
    rms = jnp.sqrt(total_sq / float(LAYERS * KV * D) + norm_eps)
    clip = jnp.minimum(1.0, 1.0 / rms)

    for name in ("master", "mcode", "scode", "mscale", "sscale"):
        loads[name].wait()
    diagonal = lax.broadcasted_iota(jnp.int32, (ROWS, 128), 0) == lax.broadcasted_iota(
        jnp.int32, (ROWS, 128), 1
    )
    diagonal_in = diagonal[:, :ROWS]

    def to_row(column):
        return jnp.sum(jnp.where(diagonal, column, 0.0), axis=0, keepdims=True)

    def to_column(row):
        return jnp.sum(jnp.where(diagonal_in, row, 0.0), axis=1, keepdims=True)

    def own_block(scales, d):
        mine = lax.broadcasted_iota(jnp.int32, (NY, ROWS), 0) == y
        return to_column(jnp.sum(jnp.where(mine, scales[d], 0.0), axis=0, keepdims=True))

    rows = []
    for d in range(LAYERS):
        moment_scale = own_block(mscale, d)
        square_scale = own_block(sscale, d)
        old_moment = mcode[d].astype(F32) * moment_scale
        old_square = scode[d].astype(F32) * square_scale
        grad_now = clip * grad[d]
        moment = beta_one * old_moment + (1.0 - beta_one) * grad_now
        square = beta_two * old_square + (1.0 - beta_two) * grad_now * grad_now
        mom[d] = moment
        sqr[d] = square
        rows.append(to_row(jnp.max(jnp.abs(moment), axis=1, keepdims=True)))
        rows.append(to_row(jnp.max(square, axis=1, keepdims=True)))
    top = jnp.concatenate(rows + [jnp.zeros((4, 128), F32)], axis=0)

    top_send[...] = top
    copy = pltpu.make_async_remote_copy(
        src_ref=top_send, dst_ref=top_recv, send_sem=top_sems.at[0], recv_sem=top_sems.at[1],
        device_id={"core": 1 - c}, device_id_type=MESH,
    )
    copy.start()
    started.append(copy)
    copy.wait_recv()
    top = jnp.maximum(top, top_recv[...])
    gather[y] = top
    copies = []
    for i in range(1, NY):
        copy = pltpu.make_async_remote_copy(
            src_ref=gather.at[y], dst_ref=gather.at[y],
            send_sem=gather_send_sems.at[i - 1], recv_sem=gather_recv_sems.at[i - 1],
            device_id={"y": wrap(y + i, NY)}, device_id_type=MESH,
        )
        copy.start()
        started.append(copy)
        incoming = gather.at[wrap(y - i, NY)]
        copies.append(pltpu.make_async_remote_copy(
            src_ref=incoming, dst_ref=incoming,
            send_sem=gather_send_sems.at[i - 1], recv_sem=gather_recv_sems.at[i - 1],
            device_id={"y": wrap(y + i, NY)}, device_id_type=MESH,
        ))

    correct_one = 1.0 - beta_one**STEP
    correct_two = 1.0 - beta_two**STEP
    for d in range(LAYERS):
        moment_div = to_column(top[2 * d : 2 * d + 1, :ROWS]) + scale_eps
        square_div = to_column(top[2 * d + 1 : 2 * d + 2, :ROWS]) + scale_eps
        moment = mom[d]
        square = sqr[d]
        mcode_out[d] = (moment / moment_div).astype(jnp.bfloat16)
        scode_out[d] = (square / square_div).astype(jnp.bfloat16)
        ratio = moment / correct_one / (jnp.sqrt(square / correct_two) + adam_eps)
        weights = master[d]
        weights_out[d] = weights - learn_rate * (decay_rate * weights + ratio)

    for copy in copies:
        copy.wait_recv()
    for b in range(NY):
        for d in range(LAYERS):
            mscale_out[d, b : b + 1, :] = gather[b, 2 * d : 2 * d + 1, :ROWS]
            sscale_out[d, b : b + 1, :] = gather[b, 2 * d + 1 : 2 * d + 2, :ROWS]
    for copy in started:
        copy.wait_send()


def local(
    activations, cotangent, master_weights, moment_codes, square_codes, moment_scales, square_scales
):
    shard = (LAYERS, ROWS, COLS)
    scales = (LAYERS, NY, ROWS)
    any_spec = pl.BlockSpec(memory_space=pl.ANY)
    vmem_spec = pl.BlockSpec(memory_space=pltpu.VMEM)
    sems = pltpu.SemaphoreType.DMA
    n_norm = (NY * NC - 1) + (NX - 1) + (NZ - 1)
    outs = pl.pallas_call(
        kernel,
        out_shape=(
            jax.ShapeDtypeStruct(shard, F32),
            jax.ShapeDtypeStruct(shard, jnp.bfloat16),
            jax.ShapeDtypeStruct(shard, jnp.bfloat16),
            jax.ShapeDtypeStruct(scales, F32),
            jax.ShapeDtypeStruct(scales, F32),
        ),
        in_specs=[any_spec] * 7,
        out_specs=[vmem_spec] * 5,
        scratch_shapes=[
            pltpu.VMEM((LAYERS, TOK, COLS), jnp.bfloat16),
            pltpu.VMEM((LAYERS, NX, TOK, XROWS), jnp.bfloat16),
            pltpu.VMEM(shard, F32),
            pltpu.VMEM(shard, jnp.bfloat16),
            pltpu.VMEM(shard, jnp.bfloat16),
            pltpu.VMEM(scales, F32),
            pltpu.VMEM(scales, F32),
            pltpu.VMEM((LAYERS, NX, XROWS, COLS), F32),
            pltpu.VMEM((2, NZ * (NX - 1), ROWS, CA), F32),
            pltpu.VMEM((2, NZ - 1, ROWS, CA), F32),
            pltpu.VMEM((2, NX * (NZ - 1), ROWS, CB), F32),
            pltpu.VMEM((2, NX - 1, ROWS, CB), F32),
            pltpu.VMEM(shard, F32),
            pltpu.VMEM(shard, F32),
            pltpu.VMEM(shard, F32),
            pltpu.VMEM((3, 1, 128), F32),
            pltpu.VMEM((n_norm, 1, 128), F32),
            pltpu.VMEM((8, 128), F32),
            pltpu.VMEM((8, 128), F32),
            pltpu.VMEM((NY, 8, 128), F32),
            sems((2 * (NX + 1) + 5,)),
            sems((2, NZ * (NX - 1))), sems((2, NZ * (NX - 1))),
            sems((2, NZ - 1)), sems((2, NZ - 1)),
            sems((2, NX * (NZ - 1))), sems((2, NX * (NZ - 1))),
            sems((2, NX - 1)), sems((2, NX - 1)),
            sems((n_norm,)), sems((n_norm,)), sems((2,)), sems((NY - 1,)), sems((NY - 1,)),
        ],
        compiler_params=pltpu.CompilerParams(
            collective_id=0, has_side_effects=True, vmem_limit_bytes=60 * 1024 * 1024
        ),
    )(
        activations, cotangent, master_weights, moment_codes, square_codes,
        jnp.transpose(moment_scales, (0, 2, 1)), jnp.transpose(square_scales, (0, 2, 1)),
    )
    return (*outs[:3], jnp.transpose(outs[3], (0, 2, 1)), jnp.transpose(outs[4], (0, 2, 1)))


def solution(mesh):
    split = Mesh(mesh.devices.reshape(NX, NZ, NY, NC), ("x", "z", "y", "core"))
    dp, col = ("x", "z"), ("y", "core")
    big, scale = P(None, dp, col), P(None, dp, None)
    return jax.shard_map(
        local,
        mesh=split,
        in_specs=(big, scale, big, big, big, scale, scale),
        out_specs=(big, big, big, scale, scale),
        check_vma=False,
    )
```

time: 360 us -> 133 us (0.37)
  waiting for transfers between devices: 261 us -> 0 us
  Pallas kernels: 0 us -> 124 us
  blocking collectives: 49.3 us -> 0 us
  matrix products: 16 us -> 0 us
  between operations: 15.6 us -> 0.64 us
  other arithmetic: 6.09 us -> 0 us
  local copies, waits for them, and re-layouts: 11.8 us -> 7.76 us
    reduce_scatter x1 -> x0, waiting for transfers between devices: 154 us -> none  [summed_rows(): total = lax.psum_scatter(total, axis, scatter_dimension=0, tiled=True)]
    pallas_call x0 -> x1, Pallas kernels: none -> 124 us  [local(): pl.pallas_call(kernel, out_shape=(jax.ShapeDtypeStruct(shard, F32), jax.S...]
    unnamed x3 -> x0, waiting for transfers between devices: 107 us -> none
    psum x4 -> x0, blocking collectives: 41.9 us -> none  [by_axis(): array = lax.psum(array, axis)]
    dot_general x1 -> x0, matrix products: 16 us -> none  [local(): jnp.einsum('ltk,ltd->kld', cotangent, activations, preferred_element_type...]
    reduce_scatter x2 -> x0, local copies, waits for them, and re-layouts: 7.54 us -> none  [summed_rows(): total = lax.psum_scatter(total, axis, scatter_dimension=0, tiled=True)]
    all_to_all x1 -> x0, blocking collectives: 7.43 us -> none  [sent_to_all(): return lax.all_to_all(copies, axis, split_axis=0, concat_axis=0, tiled=True)]
    unnamed x18 -> x5, local copies, waits for them, and re-layouts: 2.68 us -> 7.76 us
  transfers between devices with their start and end apart: 2 -> 0, of which waited for: 2 -> 0; matrix products, arithmetic and copies ran while one was open for 0% -> 0% of each run, Pallas kernels for 0% -> 0%
where the time goes in v1:
time: 133 us
  Pallas kernels  124 us (93%)
  local copies, waits for them, and re-layouts  7.76 us (6%)
    pallas_call x1, Pallas kernels, local(): pl.pallas_call(kernel, out_shape=(jax.ShapeDtypeStruct(shard, F32), jax.S...  124 us
    unnamed x5, local copies, waits for them, and re-layouts  7.76 us

profile of v1, /device:TPU:1, one launch (start us, length us, event | category | flops | bytes accessed | tf_op | source)
XLA Modules:
  0.0 132.6 jit_solution(13720786969221388445)
XLA Ops:
  0.6 124.2 %shard_map.110 = (f32[2,64,1024]{2,1,0:T(8,128)}, bf16[2,64,1024]{2,1,0:T(8,128)(2,1)}, bf16[2,64,1024]{2,1,0:T(8,128)(2,1)}, f32[2,4,64]{2,1,0:T(4,128)}, f32[2,4,64]{2,1,0:T(4,128)}) custom-call(bf16[2,896,1024]{2,1,0:T(8,128)(2,1)} %act_hbm.1, bf16[2,896,2048]{2,1,0:T(8,128)(2,1)} %cot_hbm.1, f32[2,64,1024]{2,1,0:T(8,128)} %master_hbm.1, ...), custom_call_target="tpu_custom_call" | custom-call | tf_op jit(solution)/shard_map/pallas_call | solution.py:374
  124.8 1.9 %copy.17 = f32[2,64,1024]{2,1,0:T(8,128)} copy(f32[2,64,1024]{2,1,0:T(8,128)} %get-tuple-element.20) | data formatting | bytes 1048576
  126.7 1.7 %copy.18 = bf16[2,64,1024]{2,1,0:T(8,128)(2,1)} copy(bf16[2,64,1024]{2,1,0:T(8,128)(2,1)} %get-tuple-element.21) | data formatting | bytes 524288
  128.4 1.7 %copy.19 = bf16[2,64,1024]{2,1,0:T(8,128)(2,1)} copy(bf16[2,64,1024]{2,1,0:T(8,128)(2,1)} %get-tuple-element.22) | data formatting | bytes 524288
  130.1 1.3 copy.20
  131.3 1.3 copy.21

commit v2 on v1

v2 whole, which is shorter than its diff:
```python
import functools
import heapq

import jax
import jax.numpy as jnp
from jax import lax
from jax.experimental import pallas as pl
from jax.experimental.pallas import tpu as pltpu
from jax.sharding import Mesh
from jax.sharding import PartitionSpec as P

D = 8192
KV = 2048
BLOCK = 2048
LAYERS = 2
STEP = 10

beta_one = 0.9
beta_two = 0.999
learn_rate = 0.001
decay_rate = 0.1
adam_eps = 1e-08
scale_eps = 1e-06
norm_eps = 1e-06

NX, NZ, NY, NC = 4, 8, 4, 2
ROWS = KV // (NX * NZ)
COLS = D // (NY * NC)
TOK = 896
XROWS = ROWS * NZ
TILES = COLS // 128
BLOCK_ROWS = TILES * ROWS
RA = 304
RB = BLOCK_ROWS - RA
WINDOW_A, WINDOW_B = 2, 4
MESH = pl.DeviceIdType.MESH
F32 = jnp.float32


def task_order(rate=44e3, latency=2.5, add=0.2, matmul=2.0):
    bytes_a, bytes_b = RA * 512, RB * 512
    now, order, free, heap, seen = 0.0, [], {}, [], set()
    matmuls = [("M", d, s, h) for s in range(NX) for d in (0, 1) for h in ((1, 0) if s == 0 else (2,))]
    arrived, count, serial = [], 0, 0
    total = 2 * (NZ * (NX - 1) + NZ - 1 + NX * (NZ - 1) + NX - 1)

    def ready(task):
        kind, d, j, s = task
        need = {
            "A": ("M", d, s + 1, 2),
            "B": ("M", d, j, 2 if j else 1),
            "ZA": ("A", d, s + 1, NX - 2),
            "XB": ("B", d, j + 1, NZ - 2),
        }[kind]
        return need in seen

    def enabled(task):
        kind, d, j, s = task
        out = []
        if kind == "M":
            if j == 0 and s == 0:
                out += [("A", d, q, 0) for q in range(WINDOW_A)]
            if j < WINDOW_B and s:
                out.append(("B", d, j, 0))
        elif kind == "A":
            if s < NX - 2:
                out.append(("A", d, j, s + 1))
            else:
                if j == 0:
                    out.append(("ZA", d, 0, 0))
                if j + WINDOW_A < NZ:
                    out.append(("A", d, j + WINDOW_A, 0))
        elif kind == "B":
            if s < NZ - 2:
                out.append(("B", d, j, s + 1))
            else:
                if j == 0:
                    out.append(("XB", d, 0, 0))
                if j + WINDOW_B < NX:
                    out.append(("B", d, j + WINDOW_B, 0))
        elif kind == "ZA":
            if s < NZ - 2:
                out.append(("ZA", d, 0, s + 1))
        elif kind == "XB":
            if j < NX - 2:
                out.append(("XB", d, j + 1, 0))
        return out

    while count < total or matmuls:
        while heap and heap[0][0] <= now:
            arrived.append(heapq.heappop(heap))
        able = [a for a in arrived if ready(a[2])]
        if able:
            first = min(able)
            arrived.remove(first)
            task = first[2]
            now += add
            count += 1
        elif matmuls:
            task = matmuls.pop(0)
            now += matmul if task[3] == 2 else matmul / 2
        else:
            now = max(now, heap[0][0])
            continue
        seen.add(task)
        sends = enabled(task)
        for send in sends:
            link = ("x" if send[0] in ("A", "XB") else "z", send[1])
            size = bytes_a if send[0] in ("A", "ZA") else bytes_b
            free[link] = max(now, free.get(link, 0.0)) + size / rate
            heapq.heappush(heap, (free[link] + latency, serial, send))
            serial += 1
        order.append((task, sends))
    return order


def kernel(
    act_hbm, cot_hbm, mcode_hbm, scode_hbm, mscale_hbm, sscale_hbm,
    grad_out, small_out,
    act, cot, cot_t, mcode, scode, mscale, sscale,
    part, buf_a, buf_za, buf_b, buf_xb, grad, old_m, old_s, norm_send, norm_recv, own_top, tops,
    in_sems, send_sems, recv_sems, recv_a, recv_za, recv_b, recv_xb, out_sems,
):
    x, z, y, c = (lax.axis_index(n) for n in ("x", "z", "y", "core"))
    sign = (1, -1)

    def wrap(v, n):
        return lax.rem(v + 2 * n, n)

    def xrel(d, s):
        return wrap(x - sign[d] * (1 + s), NX)

    def zrel(d, s):
        return wrap(z - sign[d] * (1 + s), NZ)

    loads = {}

    def load(name, src, dst, k):
        loads[name] = pltpu.make_async_copy(src, dst, in_sems.at[k])
        loads[name].start()

    def cot_columns(d, s):
        return pl.ds(pl.multiple_of(xrel(d, s) * XROWS, XROWS), XROWS)

    half = COLS // 2
    groups = []
    for s in range(NX):
        for d in (0, 1):
            group = [(("cot", d, s), cot_hbm.at[d, :, cot_columns(d, s)], cot.at[d, s])]
            if s == 0:
                for h in (1, 0):
                    group.append((("act", d, h), act_hbm.at[d, :, pl.ds(h * half, half)], act.at[d, h]))
            groups.append(group)
    groups.append([
        ("mcode", mcode_hbm, mcode), ("scode", scode_hbm, scode),
        ("mscale", mscale_hbm, mscale), ("sscale", sscale_hbm, sscale),
    ])

    def load_next():
        if groups:
            for name, src, dst in groups.pop(0):
                load(name, src, dst, len(loads))

    load_next()
    col_steps = [(i, j) for i in range(NY) for j in range(NC) if i or j]
    barrier = pltpu.get_barrier_semaphore()
    col_peers = [{"y": wrap(y + i, NY), "core": wrap(c + j, NC)} for i, j in col_steps]
    plane_peers = [
        {"x": wrap(x + i, NX), "z": wrap(z + j, NZ)} for i in range(NX) for j in range(NZ) if i or j
    ]
    stages = (col_peers, plane_peers)
    peers = [{"x": wrap(x + i, NX)} for i in sign] + [{"z": wrap(z + i, NZ)} for i in sign] + col_peers
    for peer in peers:
        pl.semaphore_signal(barrier, inc=1, device_id=peer, device_id_type=MESH)

    def own_a(d, j, s):
        return part.at[d, s, zrel(d, j), pl.ds(0, RA)]

    def own_b(d, j, s):
        return part.at[d, j, zrel(d, s), pl.ds(RA, RB)]

    def copy_of(task):
        kind, d, j, s = task
        if kind == "A":
            i = j * (NX - 1) + s
            src = own_a(d, j, 0) if s == 0 else buf_a.at[d, i - 1]
            dst, ssem, rsem, axis = buf_a.at[d, i], send_sems.at[0], recv_a.at[d, j % 4, s], "x"
        elif kind == "ZA":
            src = buf_a.at[d, NX - 2] if s == 0 else buf_za.at[d, s - 1]
            dst, ssem, rsem, axis = buf_za.at[d, s], send_sems.at[1], recv_za.at[d, s], "z"
        elif kind == "B":
            i = j * (NZ - 1) + s
            src = own_b(d, j, 0) if s == 0 else buf_b.at[d, i - 1]
            dst, ssem, rsem, axis = buf_b.at[d, i], send_sems.at[2], recv_b.at[d, i], "z"
        else:
            src = buf_b.at[d, NZ - 2] if j == 0 else buf_xb.at[d, j - 1]
            dst, ssem, rsem, axis = buf_xb.at[d, j], send_sems.at[3], recv_xb.at[d, j], "x"
        target = wrap(x + sign[d], NX) if axis == "x" else wrap(z + sign[d], NZ)
        return pltpu.make_async_remote_copy(
            src_ref=src, dst_ref=dst, send_sem=ssem, recv_sem=rsem,
            device_id={axis: target}, device_id_type=MESH,
        )

    def add_own(task):
        kind, d, j, s = task
        if kind == "A":
            i = j * (NX - 1) + s
            buf_a[d, i] = buf_a[d, i] + own_a(d, j, s + 1)[...]
        elif kind == "ZA":
            mine = buf_a[d, (s + 1) * (NX - 1) + NX - 2]
            if s == NZ - 2:
                grad[d, :RA] = buf_za[d, s] + mine
            else:
                buf_za[d, s] = buf_za[d, s] + mine
        elif kind == "B":
            i = j * (NZ - 1) + s
            buf_b[d, i] = buf_b[d, i] + own_b(d, j, s + 1)[...]
        else:
            mine = buf_b[d, (j + 1) * (NZ - 1) + NZ - 2]
            if j == NX - 2:
                grad[d, RA:] = buf_xb[d, j] + mine
            else:
                buf_xb[d, j] = buf_xb[d, j] + mine

    def product(d, s, h, start):
        out = jnp.dot(cot_t[...], act[d, h], preferred_element_type=F32)
        for t in range(TILES // 2):
            rows = pl.ds(start + t * ROWS, ROWS)
            for q in range(NZ):
                part[d, s, q, rows] = out[q * ROWS : (q + 1) * ROWS, t * 128 : (t + 1) * 128]

    half_rows = BLOCK_ROWS // 2

    def matmul(d, s, h):
        if s == 0:
            loads[("act", d, h)].wait()
        if h:
            loads[("cot", d, s)].wait()
            cot_t[...] = jnp.transpose(cot[d, s])
        if h != 1:
            load_next()
        if h == 2:

            @pl.loop(0, 2)
            def _(n):
                product(d, s, n, pl.multiple_of(n * half_rows, half_rows))
        else:
            product(d, s, h, h * half_rows)

    def old_state():
        for name in ("mcode", "scode", "mscale", "sscale"):
            loads[name].wait()
        for d in range(LAYERS):
            moment_scale = own_block(mscale[d], y)
            square_scale = own_block(sscale[d], y)
            for t in range(TILES):
                rows, cols = pl.ds(t * ROWS, ROWS), pl.ds(t * 128, 128)
                old_m[d, rows] = beta_one * (mcode[d, :, cols].astype(F32) * moment_scale)
                old_s[d, rows] = beta_two * (scode[d, :, cols].astype(F32) * square_scale)

    first = True
    for task, sends in task_order():
        if task[0] == "M":
            matmul(task[1], task[2], task[3])
            if first:
                pl.semaphore_wait(barrier, len(peers))
                first = False
        else:
            copy_of(task).wait_recv()
            add_own(task)
        for send in sends:
            copy_of(send).start()
        if task == ("M", 1, NX - 1, 2):
            old_state()

    grad_copies = [pltpu.make_async_copy(grad.at[d], grad_out.at[d], out_sems.at[d]) for d in range(LAYERS)]
    for copy in grad_copies:
        copy.start()

    lanes = [jnp.zeros((8, 128), F32) for _ in range(8)]
    for d in range(LAYERS):
        for i in range(BLOCK_ROWS // 8):
            v = grad[d, i * 8 : (i + 1) * 8, :]
            lanes[i % 8] = lanes[i % 8] + v * v
    while len(lanes) > 1:
        lanes = [p + q for p, q in zip(lanes[::2], lanes[1::2])]
    line = jnp.sum(lanes[0], axis=0, keepdims=True)
    def all_of(ref, k):
        return pltpu.make_async_remote_copy(
            src_ref=ref, dst_ref=ref, send_sem=send_sems.at[k], recv_sem=recv_sems.at[max(k - 4, 0)],
            device_id={"core": 1 - c}, device_id_type=MESH,
        )

    base = 0
    for n, stage in enumerate(stages):
        norm_send[n] = line
        for i, peer in enumerate(stage):
            pltpu.make_async_remote_copy(
                src_ref=norm_send.at[n], dst_ref=norm_recv.at[base + i],
                send_sem=send_sems.at[4 + n], recv_sem=recv_sems.at[n],
                device_id=peer, device_id_type=MESH,
            ).start()
        if n == 0:
            for k, buf in enumerate((buf_a, buf_za, buf_b, buf_xb)):
                all_of(buf, k).wait_send()
        incoming = all_of(norm_recv.at[pl.ds(base, len(stage))], 4 + n)
        incoming.wait_recv()
        sums = [norm_recv[base + i] for i in range(len(stage))]
        while len(sums) > 1:
            sums = [sum(sums[i : i + 2]) for i in range(0, len(sums), 2)]
        line = line + sums[0]
        base += len(stage)
    total_sq = jnp.sum(line, axis=1, keepdims=True)
    rms = jnp.sqrt(total_sq / float(LAYERS * KV * D) + norm_eps)
    clip = jnp.minimum(1.0, 1.0 / rms)

    rows = []
    for d in range(LAYERS):
        top_moment = jnp.zeros((ROWS, 128), F32)
        top_square = jnp.zeros((ROWS, 128), F32)
        for t in range(TILES):
            moment, square = moments(
                clip, grad[d, t * ROWS : (t + 1) * ROWS, :],
                old_m[d, t * ROWS : (t + 1) * ROWS, :], old_s[d, t * ROWS : (t + 1) * ROWS, :],
            )
            top_moment = jnp.maximum(top_moment, jnp.abs(moment))
            top_square = jnp.maximum(top_square, square)
        rows.append(to_row(jnp.max(top_moment, axis=1, keepdims=True)))
        rows.append(to_row(jnp.max(top_square, axis=1, keepdims=True)))
    top = jnp.concatenate(rows + [jnp.zeros((4, 128), F32)], axis=0)

    own_top[...] = top
    for i, ((dy, dc), peer) in enumerate(zip(col_steps, col_peers)):
        pltpu.make_async_remote_copy(
            src_ref=own_top, dst_ref=tops.at[i], send_sem=send_sems.at[6], recv_sem=recv_sems.at[2],
            device_id=peer, device_id_type=MESH,
        ).start()
    for n, stage in enumerate(stages):
        all_of(norm_recv.at[pl.ds(0, len(stage))], 4 + n).wait_send()
    for copy in grad_copies:
        copy.wait()
    incoming = all_of(tops, 6)
    incoming.wait_recv()
    same_chip = [i for i, (dy, dc) in enumerate(col_steps) if dy == 0]
    small_out[y] = jnp.maximum(top, tops[same_chip[0]])
    for dy in range(1, NY):
        pair = [tops[i] for i, step in enumerate(col_steps) if step[0] == dy]
        small_out[wrap(y - dy, NY)] = jnp.maximum(*pair)
    small_out[NY] = jnp.broadcast_to(clip, (8, 128))
    incoming.wait_send()


def to_row(column):
    diagonal = lax.broadcasted_iota(jnp.int32, (ROWS, 128), 0) == lax.broadcasted_iota(
        jnp.int32, (ROWS, 128), 1
    )
    return jnp.sum(jnp.where(diagonal, column, 0.0), axis=0, keepdims=True)


def to_column(row):
    diagonal = lax.broadcasted_iota(jnp.int32, (ROWS, ROWS), 0) == lax.broadcasted_iota(
        jnp.int32, (ROWS, ROWS), 1
    )
    return jnp.sum(jnp.where(diagonal, row, 0.0), axis=1, keepdims=True)


def own_block(scales, block):
    mine = lax.broadcasted_iota(jnp.int32, (NY, ROWS), 0) == block
    return to_column(jnp.sum(jnp.where(mine, scales, 0.0), axis=0, keepdims=True))


def moments(clip, grad, old_moment, old_square):
    grad_now = clip * grad
    moment = old_moment + (1.0 - beta_one) * grad_now
    square = old_square + (1.0 - beta_two) * grad_now * grad_now
    return moment, square


def update_kernel(
    grad, small, master, mcode, scode, mscale, sscale,
    weights_out, mcode_out, scode_out, mscale_out, sscale_out,
):
    y = lax.axis_index("y")
    clip = small[NY, :1, :1]
    top = small[y]
    correct_one = 1.0 - beta_one**STEP
    correct_two = 1.0 - beta_two**STEP
    for d in range(LAYERS):
        moment_scale = own_block(mscale[d], y)
        square_scale = own_block(sscale[d], y)
        moment_div = to_column(top[2 * d : 2 * d + 1, :ROWS]) + scale_eps
        square_div = to_column(top[2 * d + 1 : 2 * d + 2, :ROWS]) + scale_eps
        for t in range(TILES):
            cols = pl.ds(t * 128, 128)
            moment, square = moments(
                clip, grad[d, t * ROWS : (t + 1) * ROWS, :],
                beta_one * (mcode[d, :, cols].astype(F32) * moment_scale),
                beta_two * (scode[d, :, cols].astype(F32) * square_scale),
            )
            mcode_out[d, :, cols] = (moment / moment_div).astype(jnp.bfloat16)
            scode_out[d, :, cols] = (square / square_div).astype(jnp.bfloat16)
            ratio = moment / correct_one / (jnp.sqrt(square / correct_two) + adam_eps)
            weights = master[d, :, cols]
            weights_out[d, :, cols] = weights - learn_rate * (decay_rate * weights + ratio)
        for b in range(NY):
            mscale_out[d, b : b + 1, :] = small[b, 2 * d : 2 * d + 1, :ROWS]
            sscale_out[d, b : b + 1, :] = small[b, 2 * d + 1 : 2 * d + 2, :ROWS]


def local(
    activations, cotangent, master_weights, moment_codes, square_codes, moment_scales, square_scales
):
    shard = (LAYERS, ROWS, COLS)
    scales = (LAYERS, NY, ROWS)
    any_spec = pl.BlockSpec(memory_space=pl.ANY)
    vmem_spec = pl.BlockSpec(memory_space=pltpu.VMEM)
    sems = pltpu.SemaphoreType.DMA
    n_norm = NX * NZ - 1 + NY * NC - 1
    block = (LAYERS, BLOCK_ROWS, 128)
    scales_in = (jnp.transpose(moment_scales, (0, 2, 1)), jnp.transpose(square_scales, (0, 2, 1)))
    grad, small = pl.pallas_call(
        kernel,
        out_shape=(
            jax.ShapeDtypeStruct(block, F32),
            jax.ShapeDtypeStruct((NY + 1, 8, 128), F32),
        ),
        in_specs=[any_spec] * 6,
        out_specs=[any_spec, vmem_spec],
        scratch_shapes=[
            pltpu.VMEM((LAYERS, 2, TOK, COLS // 2), jnp.bfloat16),
            pltpu.VMEM((LAYERS, NX, TOK, XROWS), jnp.bfloat16),
            pltpu.VMEM((XROWS, TOK), jnp.bfloat16),
            pltpu.VMEM(shard, jnp.bfloat16),
            pltpu.VMEM(shard, jnp.bfloat16),
            pltpu.VMEM(scales, F32),
            pltpu.VMEM(scales, F32),
            pltpu.VMEM((LAYERS, NX, NZ, BLOCK_ROWS, 128), F32),
            pltpu.VMEM((2, NZ * (NX - 1), RA, 128), F32),
            pltpu.VMEM((2, NZ - 1, RA, 128), F32),
            pltpu.VMEM((2, NX * (NZ - 1), RB, 128), F32),
            pltpu.VMEM((2, NX - 1, RB, 128), F32),
            pltpu.VMEM(block, F32),
            pltpu.VMEM(block, F32),
            pltpu.VMEM(block, F32),
            pltpu.VMEM((2, 1, 128), F32),
            pltpu.VMEM((n_norm, 1, 128), F32),
            pltpu.VMEM((8, 128), F32),
            pltpu.VMEM((NY * NC - 1, 8, 128), F32),
            sems((2 * (NX + 2) + 4,)), sems((7,)), sems((3,)),
            sems((2, 4, NX - 1)), sems((2, NZ - 1)), sems((2, NX * (NZ - 1))), sems((2, NX - 1)),
            sems((LAYERS,)),
        ],
        compiler_params=pltpu.CompilerParams(
            collective_id=0, has_side_effects=True, vmem_limit_bytes=58 * 1024 * 1024
        ),
    )(activations, cotangent, moment_codes, square_codes, *scales_in)
    outs = pl.pallas_call(
        update_kernel,
        out_shape=(
            jax.ShapeDtypeStruct(shard, F32),
            jax.ShapeDtypeStruct(shard, jnp.bfloat16),
            jax.ShapeDtypeStruct(shard, jnp.bfloat16),
            jax.ShapeDtypeStruct(scales, F32),
            jax.ShapeDtypeStruct(scales, F32),
        ),
        in_specs=[vmem_spec] * 7,
        out_specs=[vmem_spec] * 5,
    )(grad, small, master_weights, moment_codes, square_codes, *scales_in)
    return (*outs[:3], jnp.transpose(outs[3], (0, 2, 1)), jnp.transpose(outs[4], (0, 2, 1)))


def solution(mesh):
    split = Mesh(mesh.devices.reshape(NX, NZ, NY, NC), ("x", "z", "y", "core"))
    dp, col = ("x", "z"), ("y", "core")
    big, scale = P(None, dp, col), P(None, dp, None)
    return jax.shard_map(
        local,
        mesh=split,
        in_specs=(big, scale, big, big, big, scale, scale),
        out_specs=(big, big, big, scale, scale),
        check_vma=False,
    )
```

time: 133 us -> 123 us (0.925)
  local copies, waits for them, and re-layouts: 7.76 us -> 0 us
  Pallas kernels: 124 us -> 122 us
    unnamed x5 -> x0, local copies, waits for them, and re-layouts: 7.76 us -> none
    pallas_call x1 -> x2, Pallas kernels: 124 us -> 122 us  [the longest x1 119 us: local(): pl.pallas_call(kernel, out_shape=(jax.ShapeDtypeStruct(block, F32), jax.S...]
where the time goes in v2:
time: 123 us; the launch traced here: 122 us
  Pallas kernels  122 us (99%)
    pallas_call x1, Pallas kernels, local(): pl.pallas_call(kernel, out_shape=(jax.ShapeDtypeStruct(block, F32), jax.S...  119 us
    pallas_call x1, Pallas kernels, local(): pl.pallas_call(update_kernel, out_shape=(jax.ShapeDtypeStruct(shard, F32)...  3.11 us

profile of v2, /device:TPU:1, one launch (start us, length us, event | category | flops | bytes accessed | tf_op | source)
XLA Modules:
  0.0 122.3 jit_solution(11597947458885856489)
XLA Ops:
  0.6 118.6 %shard_map.110 = (f32[2,512,128]{2,1,0:T(8,128)}, f32[5,8,128]{2,1,0:T(8,128)}) custom-call(bf16[2,896,1024]{2,1,0:T(8,128)(2,1)} %act_hbm.1, bf16[2,896,2048]{2,1,0:T(8,128)(2,1)} %cot_hbm.1, bf16[2,64,1024]{2,1,0:T(8,128)(2,1)} %mcode.1, bf16[2,64,1024]{2,1,0:T(8,128)(2,1)} %scode.1, f32[2,4,64]{2,1,0:T(4,128)} %bitcast.4, f32[2,4,64]{2,1,0:T(4,128)} %bitcast.6), custom_call_target="tpu_custom_call" | custom-call | tf_op jit(solution)/shard_map/pallas_call | solution.py:421
  119.2 3.1 %shard_map.111 = (f32[2,64,1024]{2,1,0:T(8,128)}, bf16[2,64,1024]{2,1,0:T(8,128)(2,1)}, bf16[2,64,1024]{2,1,0:T(8,128)(2,1)}, f32[2,4,64]{2,1,0:T(4,128)}, f32[2,4,64]{2,1,0:T(4,128)}) custom-call(f32[2,512,128]{2,1,0:T(8,128)} %get-tuple-element.12.grad, f32[5,8,128]{2,1,0:T(8,128)} %get-tuple-element.13.small, f32[2,64,1024]{2,1,0:T(8,128)} %master.1, ...), custom_call_target="tpu_custom_call" | custom-call | tf_op jit(solution)/shard_map/pallas_call | solution.py:457

commit v3 on v2

--- a/solution.py
+++ b/solution.py
@@ -116,9 +116,9 @@
 
 def kernel(
     act_hbm, cot_hbm, mcode_hbm, scode_hbm, mscale_hbm, sscale_hbm,
-    grad_out, small_out,
+    grad_out, small_hbm,
     act, cot, cot_t, mcode, scode, mscale, sscale,
-    part, buf_a, buf_za, buf_b, buf_xb, grad, old_m, old_s, norm_send, norm_recv, own_top, tops,
+    part, buf_a, buf_za, buf_b, buf_xb, grad, old_m, old_s, norm_send, norm_recv, own_top, tops, small_out,
     in_sems, send_sems, recv_sems, recv_a, recv_za, recv_b, recv_xb, out_sems,
 ):
     x, z, y, c = (lax.axis_index(n) for n in ("x", "z", "y", "core"))
@@ -165,10 +165,10 @@
     col_steps = [(i, j) for i in range(NY) for j in range(NC) if i or j]
     barrier = pltpu.get_barrier_semaphore()
     col_peers = [{"y": wrap(y + i, NY), "core": wrap(c + j, NC)} for i, j in col_steps]
-    plane_peers = [
-        {"x": wrap(x + i, NX), "z": wrap(z + j, NZ)} for i in range(NX) for j in range(NZ) if i or j
-    ]
-    stages = (col_peers, plane_peers)
+    stages = (
+        [{"x": wrap(x + i, NX), "y": wrap(y + j, NY)} for i in range(NX) for j in range(NY) if i or j],
+        [{"z": wrap(z + i, NZ), "core": wrap(c + j, NC)} for i in range(NZ) for j in range(NC) if i or j],
+    )
     peers = [{"x": wrap(x + i, NX)} for i in sign] + [{"z": wrap(z + i, NZ)} for i in sign] + col_peers
     for peer in peers:
         pl.semaphore_signal(barrier, inc=1, device_id=peer, device_id_type=MESH)
@@ -347,7 +347,10 @@
         pair = [tops[i] for i, step in enumerate(col_steps) if step[0] == dy]
         small_out[wrap(y - dy, NY)] = jnp.maximum(*pair)
     small_out[NY] = jnp.broadcast_to(clip, (8, 128))
+    small_copy = pltpu.make_async_copy(small_out, small_hbm, out_sems.at[LAYERS])
+    small_copy.start()
     incoming.wait_send()
+    small_copy.wait()
 
 
 def to_row(column):
@@ -380,31 +383,30 @@
     grad, small, master, mcode, scode, mscale, sscale,
     weights_out, mcode_out, scode_out, mscale_out, sscale_out,
 ):
+    d = pl.program_id(0)
     y = lax.axis_index("y")
     clip = small[NY, :1, :1]
-    top = small[y]
     correct_one = 1.0 - beta_one**STEP
     correct_two = 1.0 - beta_two**STEP
-    for d in range(LAYERS):
-        moment_scale = own_block(mscale[d], y)
-        square_scale = own_block(sscale[d], y)
-        moment_div = to_column(top[2 * d : 2 * d + 1, :ROWS]) + scale_eps
-        square_div = to_column(top[2 * d + 1 : 2 * d + 2, :ROWS]) + scale_eps
-        for t in range(TILES):
-            cols = pl.ds(t * 128, 128)
-            moment, square = moments(
-                clip, grad[d, t * ROWS : (t + 1) * ROWS, :],
-                beta_one * (mcode[d, :, cols].astype(F32) * moment_scale),
-                beta_two * (scode[d, :, cols].astype(F32) * square_scale),
-            )
-            mcode_out[d, :, cols] = (moment / moment_div).astype(jnp.bfloat16)
-            scode_out[d, :, cols] = (square / square_div).astype(jnp.bfloat16)
-            ratio = moment / correct_one / (jnp.sqrt(square / correct_two) + adam_eps)
-            weights = master[d, :, cols]
-            weights_out[d, :, cols] = weights - learn_rate * (decay_rate * weights + ratio)
-        for b in range(NY):
-            mscale_out[d, b : b + 1, :] = small[b, 2 * d : 2 * d + 1, :ROWS]
-            sscale_out[d, b : b + 1, :] = small[b, 2 * d + 1 : 2 * d + 2, :ROWS]
+    moment_scale = own_block(mscale[d], y)
+    square_scale = own_block(sscale[d], y)
+    moment_div = to_column(small[y, pl.ds(2 * d, 1), :ROWS]) + scale_eps
+    square_div = to_column(small[y, pl.ds(2 * d + 1, 1), :ROWS]) + scale_eps
+    for t in range(TILES):
+        cols = pl.ds(t * 128, 128)
+        moment, square = moments(
+            clip, grad[d, t * ROWS : (t + 1) * ROWS, :],
+            beta_one * (mcode[d, :, cols].astype(F32) * moment_scale),
+            beta_two * (scode[d, :, cols].astype(F32) * square_scale),
+        )
+        mcode_out[0, :, cols] = (moment / moment_div).astype(jnp.bfloat16)
+        scode_out[0, :, cols] = (square / square_div).astype(jnp.bfloat16)
+        ratio = moment / correct_one / (jnp.sqrt(square / correct_two) + adam_eps)
+        weights = master[d, :, cols]
+        weights_out[0, :, cols] = weights - learn_rate * (decay_rate * weights + ratio)
+    for b in range(NY):
+        mscale_out[0, b : b + 1, :] = small[b, pl.ds(2 * d, 1), :ROWS]
+        sscale_out[0, b : b + 1, :] = small[b, pl.ds(2 * d + 1, 1), :ROWS]
 
 
 def local(
@@ -415,7 +417,7 @@
     any_spec = pl.BlockSpec(memory_space=pl.ANY)
     vmem_spec = pl.BlockSpec(memory_space=pltpu.VMEM)
     sems = pltpu.SemaphoreType.DMA
-    n_norm = NX * NZ - 1 + NY * NC - 1
+    n_norm = NX * NY - 1 + NZ * NC - 1
     block = (LAYERS, BLOCK_ROWS, 128)
     scales_in = (jnp.transpose(moment_scales, (0, 2, 1)), jnp.transpose(square_scales, (0, 2, 1)))
     grad, small = pl.pallas_call(
@@ -424,8 +426,8 @@
             jax.ShapeDtypeStruct(block, F32),
             jax.ShapeDtypeStruct((NY + 1, 8, 128), F32),
         ),
-        in_specs=[any_spec] * 6,
-        out_specs=[any_spec, vmem_spec],
+        in_specs=[pl.BlockSpec(memory_space=pltpu.HBM)] * 6,
+        out_specs=[any_spec, any_spec],
         scratch_shapes=[
             pltpu.VMEM((LAYERS, 2, TOK, COLS // 2), jnp.bfloat16),
             pltpu.VMEM((LAYERS, NX, TOK, XROWS), jnp.bfloat16),
@@ -446,14 +448,18 @@
             pltpu.VMEM((n_norm, 1, 128), F32),
             pltpu.VMEM((8, 128), F32),
             pltpu.VMEM((NY * NC - 1, 8, 128), F32),
+            pltpu.VMEM((NY + 1, 8, 128), F32),
             sems((2 * (NX + 2) + 4,)), sems((7,)), sems((3,)),
             sems((2, 4, NX - 1)), sems((2, NZ - 1)), sems((2, NX * (NZ - 1))), sems((2, NX - 1)),
-            sems((LAYERS,)),
+            sems((LAYERS + 1,)),
         ],
         compiler_params=pltpu.CompilerParams(
-            collective_id=0, has_side_effects=True, vmem_limit_bytes=58 * 1024 * 1024
+            collective_id=0, has_side_effects=True, vmem_limit_bytes=51 * 1024 * 1024
         ),
-    )(activations, cotangent, moment_codes, square_codes, *scales_in)
+    )(*(
+        pltpu.with_memory_space_constraint(a, pltpu.HBM)
+        for a in (activations, cotangent, moment_codes, square_codes, *scales_in)
+    ))
     outs = pl.pallas_call(
         update_kernel,
         out_shape=(
@@ -463,8 +469,11 @@
             jax.ShapeDtypeStruct(scales, F32),
             jax.ShapeDtypeStruct(scales, F32),
         ),
+        grid=(LAYERS,),
         in_specs=[vmem_spec] * 7,
-        out_specs=[vmem_spec] * 5,
+        out_specs=[pl.BlockSpec((1, ROWS, COLS), lambda d: (d, 0, 0))] * 3
+        + [pl.BlockSpec((1, NY, ROWS), lambda d: (d, 0, 0))] * 2,
+        compiler_params=pltpu.CompilerParams(vmem_limit_bytes=8 * 1024 * 1024),
     )(grad, small, master_weights, moment_codes, square_codes, *scales_in)
     return (*outs[:3], jnp.transpose(outs[3], (0, 2, 1)), jnp.transpose(outs[4], (0, 2, 1)))
 

time: 123 us -> 121 us (0.984)
  Pallas kernels: 122 us -> 120 us
    pallas_call x1, Pallas kernels: 3.11 us -> 1.69 us  [local(): pl.pallas_call(update_kernel, out_shape=(jax.ShapeDtypeStruct(shard, F32)...]
where the time goes in v3:
time: 121 us; the launch traced here: 120 us
  Pallas kernels  120 us (99%)
    pallas_call x1, Pallas kernels, local(): pl.pallas_call(kernel, out_shape=(jax.ShapeDtypeStruct(block, F32), jax.S...  118 us

profile of v3, /device:TPU:1, one launch (start us, length us, event | category | flops | bytes accessed | tf_op | source)
XLA Modules:
  0.0 120.4 jit_solution(10094918603794866992)
XLA Ops:
  0.6 0.0 copy-start.1
  0.6 0.0 copy-start
  0.7 0.0 copy-start.4
  0.7 0.0 copy-start.3
  0.7 0.0 copy-start.2
  0.7 118.0 %shard_map.110 = (f32[2,512,128]{2,1,0:T(8,128)S(1)}, f32[5,8,128]{2,1,0:T(8,128)S(1)}) custom-call(bf16[2,896,1024]{2,1,0:T(8,128)(2,1)} %act_hbm.1, bf16[2,896,2048]{2,1,0:T(8,128)(2,1)} %cot_hbm.1, bf16[2,64,1024]{2,1,0:T(8,128)(2,1)} %mcode.1, bf16[2,64,1024]{2,1,0:T(8,128)(2,1)} %scode.1, f32[2,4,64]{2,1,0:T(4,128)} %bitcast.4, f32[2,4,64]{2,1,0:T(4,128)} %bitcast.6), custom_call_target="tpu_custom_call" | custom-call | tf_op jit(solution)/shard_map/pallas_call | solution.py:423
  118.7 0.0 copy-done.1
  118.7 0.0 copy-done
  118.7 0.0 copy-done.4
  118.7 0.0 copy-done.3
  118.7 0.0 copy-done.2
  118.7 1.7 %shard_map.111 = (f32[2,64,1024]{2,1,0:T(8,128)}, bf16[2,64,1024]{2,1,0:T(8,128)(2,1)}, bf16[2,64,1024]{2,1,0:T(8,128)(2,1)}, f32[2,4,64]{2,1,0:T(4,128)}, f32[2,4,64]{2,1,0:T(4,128)}) custom-call(f32[2,512,128]{2,1,0:T(8,128)S(1)} %get-tuple-element.12.grad, f32[5,8,128]{2,1,0:T(8,128)S(1)} %get-tuple-element.13.small, f32[2,64,1024]{2,1,0:T(8,128)S(1)} %copy-done.2, ...), custom_call_target="tpu_custom_call" | custom-call | tf_op jit(solution)/shard_map/pallas_call | solution.py:463
Async XLA Ops:
  0.6 118.1 %copy-start.1 = (bf16[2,64,1024]{2,1,0:T(8,128)(2,1)S(1)}, bf16[2,64,1024]{2,1,0:T(8,128)(2,1)}, u32[]{:S(2)}) copy-start(bf16[2,64,1024]{2,1,0:T(8,128)(2,1)} %scode.1) | copy-start | bytes 786436
  0.6 118.1 %copy-start = (bf16[2,64,1024]{2,1,0:T(8,128)(2,1)S(1)}, bf16[2,64,1024]{2,1,0:T(8,128)(2,1)}, u32[]{:S(2)}) copy-start(bf16[2,64,1024]{2,1,0:T(8,128)(2,1)} %mcode.1) | copy-start | bytes 786436
  0.7 118.1 %copy-start.4 = (f32[2,64,4]{1,2,0:T(4,128)S(1)}, f32[2,64,4]{1,2,0:T(4,128)}, u32[]{:S(2)}) copy-start(f32[2,64,4]{1,2,0:T(4,128)} %param.13) | copy-start | bytes 6148
  0.7 118.1 %copy-start.3 = (f32[2,64,4]{1,2,0:T(4,128)S(1)}, f32[2,64,4]{1,2,0:T(4,128)}, u32[]{:S(2)}) copy-start(f32[2,64,4]{1,2,0:T(4,128)} %param.12) | copy-start | bytes 6148
  0.7 118.1 %copy-start.2 = (f32[2,64,1024]{2,1,0:T(8,128)S(1)}, f32[2,64,1024]{2,1,0:T(8,128)}, u32[]{:S(2)}) copy-start(f32[2,64,1024]{2,1,0:T(8,128)} %master.1) | copy-start | bytes 1572868

commit v4 on v3

--- a/solution.py
+++ b/solution.py
@@ -40,7 +40,8 @@
 def task_order(rate=44e3, latency=2.5, add=0.2, matmul=2.0):
     bytes_a, bytes_b = RA * 512, RB * 512
     now, order, free, heap, seen = 0.0, [], {}, [], set()
-    matmuls = [("M", d, s, h) for s in range(NX) for d in (0, 1) for h in ((1, 0) if s == 0 else (2,))]
+    matmuls = [("M", d, 0, h) for d in (0, 1) for h in (1, 0)]
+    matmuls += [("M", d, s, 2) for s in range(1, NX) for d in (0, 1)]
     arrived, count, serial = [], 0, 0
     total = 2 * (NZ * (NX - 1) + NZ - 1 + NX * (NZ - 1) + NX - 1)
 
@@ -58,9 +59,9 @@
         kind, d, j, s = task
         out = []
         if kind == "M":
-            if j == 0 and s == 0:
+            if s == 0:
                 out += [("A", d, q, 0) for q in range(WINDOW_A)]
-            if j < WINDOW_B and s:
+            elif j < WINDOW_B:
                 out.append(("B", d, j, 0))
         elif kind == "A":
             if s < NX - 2:
@@ -116,9 +117,9 @@
 
 def kernel(
     act_hbm, cot_hbm, mcode_hbm, scode_hbm, mscale_hbm, sscale_hbm,
-    grad_out, small_hbm,
+    grad_out, small_out,
     act, cot, cot_t, mcode, scode, mscale, sscale,
-    part, buf_a, buf_za, buf_b, buf_xb, grad, old_m, old_s, norm_send, norm_recv, own_top, tops, small_out,
+    part, buf_a, buf_za, buf_b, buf_xb, grad, old_m, old_s, norm_send, norm_recv, own_top,
     in_sems, send_sems, recv_sems, recv_a, recv_za, recv_b, recv_xb, out_sems,
 ):
     x, z, y, c = (lax.axis_index(n) for n in ("x", "z", "y", "core"))
@@ -143,14 +144,15 @@
         return pl.ds(pl.multiple_of(xrel(d, s) * XROWS, XROWS), XROWS)
 
     half = COLS // 2
-    groups = []
-    for s in range(NX):
-        for d in (0, 1):
-            group = [(("cot", d, s), cot_hbm.at[d, :, cot_columns(d, s)], cot.at[d, s])]
-            if s == 0:
-                for h in (1, 0):
-                    group.append((("act", d, h), act_hbm.at[d, :, pl.ds(h * half, half)], act.at[d, h]))
-            groups.append(group)
+
+    def cot_load(d, s):
+        return (("cot", d, s), cot_hbm.at[d, :, cot_columns(d, s)], cot.at[d, s])
+
+    def act_load(d, h):
+        return (("act", d, h), act_hbm.at[d, :, pl.ds(h * half, half)], act.at[d, h])
+
+    groups = [[cot_load(d, 0), act_load(d, 1), act_load(d, 0)] for d in (0, 1)]
+    groups += [[cot_load(d, s)] for s in range(1, NX) for d in (0, 1)]
     groups.append([
         ("mcode", mcode_hbm, mcode), ("scode", scode_hbm, scode),
         ("mscale", mscale_hbm, mscale), ("sscale", sscale_hbm, sscale),
@@ -162,6 +164,7 @@
                 load(name, src, dst, len(loads))
 
     load_next()
+
     col_steps = [(i, j) for i in range(NY) for j in range(NC) if i or j]
     barrier = pltpu.get_barrier_semaphore()
     col_peers = [{"y": wrap(y + i, NY), "core": wrap(c + j, NC)} for i, j in col_steps]
@@ -201,6 +204,14 @@
             device_id={axis: target}, device_id_type=MESH,
         )
 
+    squares = [jnp.zeros((8, 128), F32) for _ in range(4)]
+
+    def finish(d, row, value):
+        grad[d, row : row + value.shape[0]] = value
+        for i in range(value.shape[0] // 8):
+            v = value[i * 8 : (i + 1) * 8, :]
+            squares[i % 4] = squares[i % 4] + v * v
+
     def add_own(task):
         kind, d, j, s = task
         if kind == "A":
@@ -209,7 +220,7 @@
         elif kind == "ZA":
             mine = buf_a[d, (s + 1) * (NX - 1) + NX - 2]
             if s == NZ - 2:
-                grad[d, :RA] = buf_za[d, s] + mine
+                finish(d, 0, buf_za[d, s] + mine)
             else:
                 buf_za[d, s] = buf_za[d, s] + mine
         elif kind == "B":
@@ -218,12 +229,12 @@
         else:
             mine = buf_b[d, (j + 1) * (NZ - 1) + NZ - 2]
             if j == NX - 2:
-                grad[d, RA:] = buf_xb[d, j] + mine
+                finish(d, RA, buf_xb[d, j] + mine)
             else:
                 buf_xb[d, j] = buf_xb[d, j] + mine
 
     def product(d, s, h, start):
-        out = jnp.dot(cot_t[...], act[d, h], preferred_element_type=F32)
+        out = jnp.dot(cot_t[d], act[d, h], preferred_element_type=F32)
         for t in range(TILES // 2):
             rows = pl.ds(start + t * ROWS, ROWS)
             for q in range(NZ):
@@ -236,9 +247,9 @@
             loads[("act", d, h)].wait()
         if h:
             loads[("cot", d, s)].wait()
-            cot_t[...] = jnp.transpose(cot[d, s])
-        if h != 1:
-            load_next()
+        load_next()
+        if h:
+            cot_t[d] = jnp.transpose(cot[d, s])
         if h == 2:
 
             @pl.loop(0, 2)
@@ -277,11 +288,7 @@
     for copy in grad_copies:
         copy.start()
 
-    lanes = [jnp.zeros((8, 128), F32) for _ in range(8)]
-    for d in range(LAYERS):
-        for i in range(BLOCK_ROWS // 8):
-            v = grad[d, i * 8 : (i + 1) * 8, :]
-            lanes[i % 8] = lanes[i % 8] + v * v
+    lanes = squares
     while len(lanes) > 1:
         lanes = [p + q for p, q in zip(lanes[::2], lanes[1::2])]
     line = jnp.sum(lanes[0], axis=0, keepdims=True)
@@ -327,30 +334,27 @@
             top_square = jnp.maximum(top_square, square)
         rows.append(to_row(jnp.max(top_moment, axis=1, keepdims=True)))
         rows.append(to_row(jnp.max(top_square, axis=1, keepdims=True)))
-    top = jnp.concatenate(rows + [jnp.zeros((4, 128), F32)], axis=0)
-
-    own_top[...] = top
-    for i, ((dy, dc), peer) in enumerate(zip(col_steps, col_peers)):
+    own_top[0] = jnp.concatenate(rows + [jnp.zeros((4, 128), F32)], axis=0)
+    own_top[1] = jnp.broadcast_to(clip, (8, 128))
+    for peer in col_peers:
         pltpu.make_async_remote_copy(
-            src_ref=own_top, dst_ref=tops.at[i], send_sem=send_sems.at[6], recv_sem=recv_sems.at[2],
+            src_ref=own_top.at[0], dst_ref=small_out.at[y * NC + c],
+            send_sem=send_sems.at[6], recv_sem=recv_sems.at[2],
             device_id=peer, device_id_type=MESH,
         ).start()
+    own_copies = [
+        pltpu.make_async_copy(own_top.at[0], small_out.at[y * NC + c], out_sems.at[LAYERS]),
+        pltpu.make_async_copy(own_top.at[1], small_out.at[NY * NC], out_sems.at[LAYERS + 1]),
+    ]
+    for copy in own_copies:
+        copy.start()
     for n, stage in enumerate(stages):
         all_of(norm_recv.at[pl.ds(0, len(stage))], 4 + n).wait_send()
-    for copy in grad_copies:
+    for copy in grad_copies + own_copies:
         copy.wait()
-    incoming = all_of(tops, 6)
+    incoming = all_of(small_out.at[pl.ds(0, NY * NC - 1)], 6)
+    incoming.wait_send()
     incoming.wait_recv()
-    same_chip = [i for i, (dy, dc) in enumerate(col_steps) if dy == 0]
-    small_out[y] = jnp.maximum(top, tops[same_chip[0]])
-    for dy in range(1, NY):
-        pair = [tops[i] for i, step in enumerate(col_steps) if step[0] == dy]
-        small_out[wrap(y - dy, NY)] = jnp.maximum(*pair)
-    small_out[NY] = jnp.broadcast_to(clip, (8, 128))
-    small_copy = pltpu.make_async_copy(small_out, small_hbm, out_sems.at[LAYERS])
-    small_copy.start()
-    incoming.wait_send()
-    small_copy.wait()
 
 
 def to_row(column):
@@ -385,13 +389,18 @@
 ):
     d = pl.program_id(0)
     y = lax.axis_index("y")
-    clip = small[NY, :1, :1]
+    clip = small[NY * NC, :1, :1]
+
+    def top(b, kind):
+        row = pl.ds(2 * d + kind, 1)
+        return jnp.maximum(small[b * NC, row, :ROWS], small[b * NC + 1, row, :ROWS])
+
     correct_one = 1.0 - beta_one**STEP
     correct_two = 1.0 - beta_two**STEP
     moment_scale = own_block(mscale[d], y)
     square_scale = own_block(sscale[d], y)
-    moment_div = to_column(small[y, pl.ds(2 * d, 1), :ROWS]) + scale_eps
-    square_div = to_column(small[y, pl.ds(2 * d + 1, 1), :ROWS]) + scale_eps
+    moment_div = to_column(top(y, 0)) + scale_eps
+    square_div = to_column(top(y, 1)) + scale_eps
     for t in range(TILES):
         cols = pl.ds(t * 128, 128)
         moment, square = moments(
@@ -405,8 +414,8 @@
         weights = master[d, :, cols]
         weights_out[0, :, cols] = weights - learn_rate * (decay_rate * weights + ratio)
     for b in range(NY):
-        mscale_out[0, b : b + 1, :] = small[b, pl.ds(2 * d, 1), :ROWS]
-        sscale_out[0, b : b + 1, :] = small[b, pl.ds(2 * d + 1, 1), :ROWS]
+        mscale_out[0, b : b + 1, :] = top(b, 0)
+        sscale_out[0, b : b + 1, :] = top(b, 1)
 
 
 def local(
@@ -424,14 +433,14 @@
         kernel,
         out_shape=(
             jax.ShapeDtypeStruct(block, F32),
-            jax.ShapeDtypeStruct((NY + 1, 8, 128), F32),
+            jax.ShapeDtypeStruct((NY * NC + 1, 8, 128), F32),
         ),
         in_specs=[pl.BlockSpec(memory_space=pltpu.HBM)] * 6,
         out_specs=[any_spec, any_spec],
         scratch_shapes=[
             pltpu.VMEM((LAYERS, 2, TOK, COLS // 2), jnp.bfloat16),
             pltpu.VMEM((LAYERS, NX, TOK, XROWS), jnp.bfloat16),
-            pltpu.VMEM((XROWS, TOK), jnp.bfloat16),
+            pltpu.VMEM((LAYERS, XROWS, TOK), jnp.bfloat16),
             pltpu.VMEM(shard, jnp.bfloat16),
             pltpu.VMEM(shard, jnp.bfloat16),
             pltpu.VMEM(scales, F32),
@@ -446,12 +455,10 @@
             pltpu.VMEM(block, F32),
             pltpu.VMEM((2, 1, 128), F32),
             pltpu.VMEM((n_norm, 1, 128), F32),
-            pltpu.VMEM((8, 128), F32),
-            pltpu.VMEM((NY * NC - 1, 8, 128), F32),
-            pltpu.VMEM((NY + 1, 8, 128), F32),
+            pltpu.VMEM((2, 8, 128), F32),
             sems((2 * (NX + 2) + 4,)), sems((7,)), sems((3,)),
             sems((2, 4, NX - 1)), sems((2, NZ - 1)), sems((2, NX * (NZ - 1))), sems((2, NX - 1)),
-            sems((LAYERS + 1,)),
+            sems((LAYERS + 2,)),
         ],
         compiler_params=pltpu.CompilerParams(
             collective_id=0, has_side_effects=True, vmem_limit_bytes=51 * 1024 * 1024

time: 121 us -> 119 us (0.983)
  Pallas kernels: 120 us -> 118 us
    pallas_call x1, Pallas kernels: 118 us -> 117 us  [local(): pl.pallas_call(kernel, out_shape=(jax.ShapeDtypeStruct(block, F32), jax.S...]
where the time goes in v4:
time: 119 us
  Pallas kernels  118 us (99%)
    pallas_call x1, Pallas kernels, local(): pl.pallas_call(kernel, out_shape=(jax.ShapeDtypeStruct(block, F32), jax.S...  117 us

profile of v4, /device:TPU:1, one launch (start us, length us, event | category | flops | bytes accessed | tf_op | source)
XLA Modules:
  0.0 119.2 jit_solution(8911125412499157756)
XLA Ops:
  0.6 0.0 copy-start.1
  0.6 0.0 copy-start
  0.7 0.0 copy-start.4
  0.7 0.0 copy-start.3
  0.7 0.0 copy-start.2
  0.7 116.7 %shard_map.110 = (f32[2,512,128]{2,1,0:T(8,128)S(1)}, f32[9,8,128]{2,1,0:T(8,128)S(1)}) custom-call(bf16[2,896,1024]{2,1,0:T(8,128)(2,1)} %act_hbm.1, bf16[2,896,2048]{2,1,0:T(8,128)(2,1)} %cot_hbm.1, bf16[2,64,1024]{2,1,0:T(8,128)(2,1)} %mcode.1, bf16[2,64,1024]{2,1,0:T(8,128)(2,1)} %scode.1, f32[2,4,64]{2,1,0:T(4,128)} %bitcast.4, f32[2,4,64]{2,1,0:T(4,128)} %bitcast.6), custom_call_target="tpu_custom_call" | custom-call | tf_op jit(solution)/shard_map/pallas_call | solution.py:432
  117.4 0.0 copy-done.1
  117.4 0.0 copy-done
  117.4 0.0 copy-done.4
  117.5 0.0 copy-done.3
  117.5 0.0 copy-done.2
  117.5 1.7 %shard_map.111 = (f32[2,64,1024]{2,1,0:T(8,128)}, bf16[2,64,1024]{2,1,0:T(8,128)(2,1)}, bf16[2,64,1024]{2,1,0:T(8,128)(2,1)}, f32[2,4,64]{2,1,0:T(4,128)}, f32[2,4,64]{2,1,0:T(4,128)}) custom-call(f32[2,512,128]{2,1,0:T(8,128)S(1)} %get-tuple-element.12.grad, f32[9,8,128]{2,1,0:T(8,128)S(1)} %get-tuple-element.13.small, f32[2,64,1024]{2,1,0:T(8,128)S(1)} %copy-done.2, ...), custom_call_target="tpu_custom_call" | custom-call | tf_op jit(solution)/shard_map/pallas_call | solution.py:470
Async XLA Ops:
  0.6 116.8 %copy-start.1 = (bf16[2,64,1024]{2,1,0:T(8,128)(2,1)S(1)}, bf16[2,64,1024]{2,1,0:T(8,128)(2,1)}, u32[]{:S(2)}) copy-start(bf16[2,64,1024]{2,1,0:T(8,128)(2,1)} %scode.1) | copy-start | bytes 786436
  0.6 116.8 %copy-start = (bf16[2,64,1024]{2,1,0:T(8,128)(2,1)S(1)}, bf16[2,64,1024]{2,1,0:T(8,128)(2,1)}, u32[]{:S(2)}) copy-start(bf16[2,64,1024]{2,1,0:T(8,128)(2,1)} %mcode.1) | copy-start | bytes 786436
  0.7 116.8 %copy-start.4 = (f32[2,64,4]{1,2,0:T(4,128)S(1)}, f32[2,64,4]{1,2,0:T(4,128)}, u32[]{:S(2)}) copy-start(f32[2,64,4]{1,2,0:T(4,128)} %param.13) | copy-start | bytes 6148
  0.7 116.8 %copy-start.3 = (f32[2,64,4]{1,2,0:T(4,128)S(1)}, f32[2,64,4]{1,2,0:T(4,128)}, u32[]{:S(2)}) copy-start(f32[2,64,4]{1,2,0:T(4,128)} %param.12) | copy-start | bytes 6148
  0.7 116.8 %copy-start.2 = (f32[2,64,1024]{2,1,0:T(8,128)S(1)}, f32[2,64,1024]{2,1,0:T(8,128)}, u32[]{:S(2)}) copy-start(f32[2,64,1024]{2,1,0:T(8,128)} %master.1) | copy-start | bytes 1572868

commit v5 on v4

--- a/solution.py
+++ b/solution.py
@@ -123,7 +123,7 @@
     in_sems, send_sems, recv_sems, recv_a, recv_za, recv_b, recv_xb, out_sems,
 ):
     x, z, y, c = (lax.axis_index(n) for n in ("x", "z", "y", "core"))
-    sign = (1, -1)
+    sign = (1 - 2 * c, 2 * c - 1)
 
     def wrap(v, n):
         return lax.rem(v + 2 * n, n)
@@ -172,7 +172,7 @@
         [{"x": wrap(x + i, NX), "y": wrap(y + j, NY)} for i in range(NX) for j in range(NY) if i or j],
         [{"z": wrap(z + i, NZ), "core": wrap(c + j, NC)} for i in range(NZ) for j in range(NC) if i or j],
     )
-    peers = [{"x": wrap(x + i, NX)} for i in sign] + [{"z": wrap(z + i, NZ)} for i in sign] + col_peers
+    peers = [{"x": wrap(x + i, NX)} for i in (1, -1)] + [{"z": wrap(z + i, NZ)} for i in (1, -1)] + col_peers
     for peer in peers:
         pl.semaphore_signal(barrier, inc=1, device_id=peer, device_id_type=MESH)
 

time: 119 us -> 119 us (level)
  no operation moved by 1% of the time
where the time goes in v5:
time: 119 us
  Pallas kernels  118 us (99%)
    pallas_call x1, Pallas kernels, local(): pl.pallas_call(kernel, out_shape=(jax.ShapeDtypeStruct(block, F32), jax.S...  116 us

profile of v5, /device:TPU:1, one launch (start us, length us, event | category | flops | bytes accessed | tf_op | source)
XLA Modules:
  0.0 118.7 jit_solution(3578160858399204142)
XLA Ops:
  0.6 0.0 copy-start.1
  0.6 0.0 copy-start
  0.7 0.0 copy-start.4
  0.7 0.0 copy-start.3
  0.7 0.0 copy-start.2
  0.7 116.3 %shard_map.110 = (f32[2,512,128]{2,1,0:T(8,128)S(1)}, f32[9,8,128]{2,1,0:T(8,128)S(1)}) custom-call(bf16[2,896,1024]{2,1,0:T(8,128)(2,1)} %act_hbm.1, bf16[2,896,2048]{2,1,0:T(8,128)(2,1)} %cot_hbm.1, bf16[2,64,1024]{2,1,0:T(8,128)(2,1)} %mcode.1, bf16[2,64,1024]{2,1,0:T(8,128)(2,1)} %scode.1, f32[2,4,64]{2,1,0:T(4,128)} %bitcast.4, f32[2,4,64]{2,1,0:T(4,128)} %bitcast.6), custom_call_target="tpu_custom_call" | custom-call | tf_op jit(solution)/shard_map/pallas_call | solution.py:432
  117.0 0.0 copy-done.1
  117.0 0.0 copy-done
  117.0 0.0 copy-done.4
  117.0 0.0 copy-done.3
  117.0 0.0 copy-done.2
  117.0 1.7 %shard_map.111 = (f32[2,64,1024]{2,1,0:T(8,128)}, bf16[2,64,1024]{2,1,0:T(8,128)(2,1)}, bf16[2,64,1024]{2,1,0:T(8,128)(2,1)}, f32[2,4,64]{2,1,0:T(4,128)}, f32[2,4,64]{2,1,0:T(4,128)}) custom-call(f32[2,512,128]{2,1,0:T(8,128)S(1)} %get-tuple-element.12.grad, f32[9,8,128]{2,1,0:T(8,128)S(1)} %get-tuple-element.13.small, f32[2,64,1024]{2,1,0:T(8,128)S(1)} %copy-done.2, ...), custom_call_target="tpu_custom_call" | custom-call | tf_op jit(solution)/shard_map/pallas_call | solution.py:470
Async XLA Ops:
  0.6 116.3 %copy-start.1 = (bf16[2,64,1024]{2,1,0:T(8,128)(2,1)S(1)}, bf16[2,64,1024]{2,1,0:T(8,128)(2,1)}, u32[]{:S(2)}) copy-start(bf16[2,64,1024]{2,1,0:T(8,128)(2,1)} %scode.1) | copy-start | bytes 786436
  0.6 116.3 %copy-start = (bf16[2,64,1024]{2,1,0:T(8,128)(2,1)S(1)}, bf16[2,64,1024]{2,1,0:T(8,128)(2,1)}, u32[]{:S(2)}) copy-start(bf16[2,64,1024]{2,1,0:T(8,128)(2,1)} %mcode.1) | copy-start | bytes 786436
  0.7 116.3 %copy-start.4 = (f32[2,64,4]{1,2,0:T(4,128)S(1)}, f32[2,64,4]{1,2,0:T(4,128)}, u32[]{:S(2)}) copy-start(f32[2,64,4]{1,2,0:T(4,128)} %param.13) | copy-start | bytes 6148
  0.7 116.3 %copy-start.3 = (f32[2,64,4]{1,2,0:T(4,128)S(1)}, f32[2,64,4]{1,2,0:T(4,128)}, u32[]{:S(2)}) copy-start(f32[2,64,4]{1,2,0:T(4,128)} %param.12) | copy-start | bytes 6148
  0.7 116.3 %copy-start.2 = (f32[2,64,1024]{2,1,0:T(8,128)S(1)}, f32[2,64,1024]{2,1,0:T(8,128)}, u32[]{:S(2)}) copy-start(f32[2,64,1024]{2,1,0:T(8,128)} %master.1) | copy-start | bytes 1572868
